TPU v7x, 32 devices: a whole 2x2x4 slice. The times are simulated.
32 devices in a mesh: ctx: 8 (over z, x), rep: 4 (over y, core).
Axes of the slice: x: 2, y: 2, z: 4, core: 2. Of those that a mesh axis runs over, the one named last changes fastest.
Arguments:
- latents: bfloat16 [131072, 576], P(('ctx', 'rep')), may hold values from -6 to 6
- queries: bfloat16 [64, 73728], P('rep', 'ctx'), may hold values from -4000 to 4000, as said below
- hot_ids: int32 [16], P('ctx'), may hold values from 0 to 15, as said below
- lengths: int32 [64], P('rep'), may hold values from 65536 to 131072
Outputs:
- attended: bfloat16 [64, 65536], P('rep', 'ctx')
Inputs may be any that keep to these rules, and one draw needn't show every extreme that they name: `queries`: query entries lie in the stated range. `hot_ids`: entries g * 2 to (g + 1) * 2 - 1 are distinct block numbers within group g.
All inputs are finite; a program needn't handle non-finite values.
Results may differ from a plain program's by a relative error of at most 0.0031.
Values may be sent and summed in bfloat16 or wider, within the bound.
A program may use at most 128 MiB of HBM per device.

v0:
```python
import jax
import jax.numpy as jnp
from jax import lax
from jax.sharding import PartitionSpec as P

H = 128
LAT = 512
ROPE = 64
QK = 192
BLK = 1024
HOT_GRP = 2


def from_root(block, axis, holder):
    block = jnp.where(lax.axis_index(axis) == holder, block, jnp.zeros_like(block))
    return lax.psum(block, axis)


def on_device(latents, queries, hot_ids, lengths):
    row_width = LAT + ROPE
    score_scale = QK ** (-0.5)
    rep_count = lax.axis_size("rep")
    group_index = lax.axis_index("ctx")
    per_device = latents.shape[0] // BLK
    blocks_held = []
    for slot_index in range(HOT_GRP):
        owner_index = hot_ids[slot_index] // per_device
        local_block = lax.dynamic_slice_in_dim(
            latents, hot_ids[slot_index] % per_device * BLK, BLK, 0
        )
        blocks_held.append(from_root(local_block, "rep", owner_index))
    key_rows = jnp.concatenate(blocks_held, axis=0)
    value_rows = key_rows[:, :LAT]
    offsets = jnp.arange(BLK, dtype=jnp.int32)
    row_index = (
        (group_index * (rep_count * per_device) + hot_ids)[:, None] * BLK + offsets[None, :]
    ).reshape(-1)
    all_heads = lax.all_gather(queries, "ctx", axis=1, tiled=True)
    query_count = all_heads.shape[0]
    query_blocks = all_heads.reshape(query_count // 4, 4, H, row_width)
    span_blocks = lengths.reshape(query_count // 4, 4)

    def partial_value(item_pair):
        query_block, span_block = item_pair
        scores = (
            jnp.einsum("qhw,kw->qhk", query_block, key_rows, preferred_element_type=jnp.float32)
            * score_scale
        )
        visible = row_index[None, None, :] < span_block[:, None, None]
        peak_score = jnp.max(jnp.where(visible, scores, -1e30), axis=2)
        exponent = jnp.where(visible, scores - peak_score[:, :, None], -1e30)
        weights = jnp.exp(exponent).astype(jnp.bfloat16)
        totals = jnp.sum(weights, axis=2, dtype=jnp.float32)
        numerators = jnp.einsum(
            "qhk,kl->qhl", weights, value_rows, preferred_element_type=jnp.float32
        )
        return (numerators, peak_score, totals)

    numerators, peak_score, totals = lax.map(partial_value, (query_blocks, span_blocks))
    numerators = numerators.reshape(query_count, H, LAT)
    peak_score = peak_score.reshape(query_count, H)
    totals = totals.reshape(query_count, H)
    all_numer, all_peak, all_total = (
        lax.all_to_all(numerators[None], "ctx", split_axis=2, concat_axis=0, tiled=True),
        lax.all_to_all(peak_score[None], "ctx", split_axis=2, concat_axis=0, tiled=True),
        lax.all_to_all(totals[None], "ctx", split_axis=2, concat_axis=0, tiled=True),
    )
    overall = jnp.max(all_peak, axis=0)
    factor = jnp.exp(all_peak - overall[None])
    merged = jnp.sum(all_numer * factor[..., None], axis=0)
    weight_sum = jnp.sum(all_total * factor, axis=0)
    return (merged / weight_sum[..., None]).reshape(query_count, -1).astype(jnp.bfloat16)


def solution(mesh):
    placed = (P(("ctx", "rep"), None), P("rep", "ctx"), P("ctx"), P("rep"))
    return jax.shard_map(
        on_device, mesh=mesh, in_specs=placed, out_specs=P("rep", "ctx"), check_vma=False
    )
```

profile of v0, /device:TPU:0, one launch (start us, length us, event | category | flops | bytes accessed | tf_op | source)
XLA Modules:
  0.0 254.2 jit_solution(5459596877738601110)
XLA Ops:
  7.4 1.4 fusion.19
  13.9 3.7 %dynamic-slice_select_fusion = (bf16[1024,576]{0,1:T(8,128)(2,1)}, bf16[1024,576]{0,1:T(8,128)(2,1)}) fusion(bf16[4096,576]{0,1:T(8,128)(2,1)} %param.6, s32[]{:T(128)S(6)} %select_n.53, pred[]{:T(512)S(6)} %eq.10, s32[]{:T(128)S(6)} %select_n.48, pred[]{:T(512)S(6)} %eq.9), kind=kLoop, calls=%fused_computation.23 | loop fusion | flops 1179648 | bytes 4718602 | tf_op jit(solution)/shard_map/jit(_where)/select_n | solution.py:15
  18.3 57.9 %all-reduce.3.cloned.1.call-done = (bf16[1024,576]{0,1:T(8,128)(2,1)}, bf16[1024,576]{0,1:T(8,128)(2,1)}) async-done(((bf16[1024,576]{0,1:T(8,128)(2,1)}, bf16[1024,576]{0,1:T(8,128)(2,1)}), (bf16[1024,576]{0,1:T(8,128)(2,1)}, bf16[1024,576]{0,1:T(8,128)(2,1)})) %all-reduce.3.cloned.1.call-update) | async-done | bytes 2359312 | tf_op jit(solution)/shard_map/psum | solution.py:16
  77.5 1.4 constant_dynamic-update-slice_fusion
  78.9 1.5 slice.14
  80.4 3.9 %copy.30 = bf16[2048,512]{1,0:T(8,128)(2,1)} copy(bf16[2048,512]{0,1:T(8,128)(2,1)} %slice.14) | data formatting | bytes 4194304
  84.3 5.5 %reshape.58 = bf16[4,4,128,576]{3,2,1,0:T(8,128)(2,1)} reshape(bf16[16,73728]{1,0:T(8,128)(2,1)} %all-gather.2.cloned.1.call-done) | data formatting | bytes 4718592 | tf_op jit(solution)/shard_map/reshape | solution.py:40
  89.8 4.4 %copy.24 = bf16[4,4,128,576]{2,3,1,0:T(8,128)(2,1)} copy(bf16[4,4,128,576]{3,2,1,0:T(8,128)(2,1)} %reshape.58) | data formatting | bytes 4718592
  94.2 27.9 %while.15 = (s32[]{:T(128)}, f32[4,4,128,512]{3,2,1,0:T(8,128)}, f32[4,4,128]{2,1,0:T(4,128)S(1)}, f32[4,4,128]{2,1,0:T(4,128)S(1)}, s32[4,4]{1,0:T(4,128)S(1)},...) while((s32[]{:T(128)}, f32[4,4,128,512]{3,2,1,0:T(8,128)}, ...), condition=%wide.region_5.6_spmd.clone, body=%wide.region_2.5_spmd.clone.sunk | while | flops 2295342080 | bytes 27149504 | solution.py:59
  94.4 3.4 %select_reduce_fusion.2 = (f32[4,128]{1,0:T(4,128)S(1)}, f32[4,128,2048]{2,1,0:T(8,128)S(1)}) fusion(pred[4,2048]{1,0:T(4,128)(4,1)S(1)} %broadcast_compare_fusion.2, bf16[2048,576]{0,1:T(8,128)(2,1)S(1)} %get-tuple-element.242, bf16[4,4,128,576]{2,3,1,0:T(8,128)(2,1)} %get-tuple-element.241, s32[]{:T(128)} %get-tuple-element.226), kind=kOutput, calls=%fused_computation.3.clone.1 | convolution fusion | flops 1211104768 | bytes 7154176 | tf_op jit(solution)/shard_map/while/body/eval_jaxpr/qhw,kw->qhk/dot_general | solution.py:46
  98.8 2.3 fusion.25
  101.3 3.4 %select_reduce_fusion.2 = (f32[4,128]{1,0:T(4,128)S(1)}, f32[4,128,2048]{2,1,0:T(8,128)S(1)}) fusion(pred[4,2048]{1,0:T(4,128)(4,1)S(1)} %broadcast_compare_fusion.2, bf16[2048,576]{0,1:T(8,128)(2,1)S(1)} %get-tuple-element.242, bf16[4,4,128,576]{2,3,1,0:T(8,128)(2,1)} %get-tuple-element.241, s32[]{:T(128)} %get-tuple-element.226), kind=kOutput, calls=%fused_computation.3.clone.1 | convolution fusion | flops 1211104768 | bytes 7154176 | tf_op jit(solution)/shard_map/while/body/eval_jaxpr/qhw,kw->qhk/dot_general | solution.py:46
  105.8 2.4 fusion.25
  108.3 3.4 %select_reduce_fusion.2 = (f32[4,128]{1,0:T(4,128)S(1)}, f32[4,128,2048]{2,1,0:T(8,128)S(1)}) fusion(pred[4,2048]{1,0:T(4,128)(4,1)S(1)} %broadcast_compare_fusion.2, bf16[2048,576]{0,1:T(8,128)(2,1)S(1)} %get-tuple-element.242, bf16[4,4,128,576]{2,3,1,0:T(8,128)(2,1)} %get-tuple-element.241, s32[]{:T(128)} %get-tuple-element.226), kind=kOutput, calls=%fused_computation.3.clone.1 | convolution fusion | flops 1211104768 | bytes 7154176 | tf_op jit(solution)/shard_map/while/body/eval_jaxpr/qhw,kw->qhk/dot_general | solution.py:46
  112.8 2.3 fusion.25
  115.3 3.4 %select_reduce_fusion.2 = (f32[4,128]{1,0:T(4,128)S(1)}, f32[4,128,2048]{2,1,0:T(8,128)S(1)}) fusion(pred[4,2048]{1,0:T(4,128)(4,1)S(1)} %broadcast_compare_fusion.2, bf16[2048,576]{0,1:T(8,128)(2,1)S(1)} %get-tuple-element.242, bf16[4,4,128,576]{2,3,1,0:T(8,128)(2,1)} %get-tuple-element.241, s32[]{:T(128)} %get-tuple-element.226), kind=kOutput, calls=%fused_computation.3.clone.1 | convolution fusion | flops 1211104768 | bytes 7154176 | tf_op jit(solution)/shard_map/while/body/eval_jaxpr/qhw,kw->qhk/dot_general | solution.py:46
  119.8 2.3 fusion.25
  124.1 5.5 %all-to-all-start.1 = ((f32[8,1,256]{2,1,0:T(1,128)}), f32[8,1,256]{2,1,0:T(1,128)S(1)}, u32[]{:S(2)}, u32[]{:S(2)}) async-start(f32[8,1,256]{2,1,0:T(1,128)} %reshape.61), calls=%async_computation.1 | async-start | bytes 16384 | tf_op jit(solution)/shard_map/all_to_all | solution.py:65
  131.1 5.0 %all-to-all-done.1 = f32[8,1,256]{2,1,0:T(1,128)S(1)} async-done(((f32[8,1,256]{2,1,0:T(1,128)}), f32[8,1,256]{2,1,0:T(1,128)S(1)}, u32[]{:S(2)}, u32[]{:S(2)}) %all-to-all-start.1) | async-done | bytes 8224 | tf_op jit(solution)/shard_map/all_to_all | solution.py:65
  136.1 3.3 %all-to-all-start.2 = ((f32[8,1,256]{2,1,0:T(1,128)}), f32[8,1,256]{2,1,0:T(1,128)S(1)}, u32[]{:S(2)}, u32[]{:S(2)}) async-start(f32[8,1,256]{2,1,0:T(1,128)} %reshape.63), calls=%async_computation.2 | async-start | bytes 16384 | tf_op jit(solution)/shard_map/all_to_all | solution.py:66
  139.5 6.6 %copy.29 = f32[1,16,128,512]{3,1,0,2:T(8,128)} copy(f32[1,16,128,512]{3,2,1,0:T(8,128)} %bitcast.2) | data formatting | bytes 8388608 | tf_op jit(solution)/shard_map/broadcast_in_dim;reshape | solution.py:64
  146.1 5.9 %all-to-all-start = ((f32[1,16,128,512]{3,1,0,2:T(8,128)}), f32[1,16,128,512]{3,1,0,2:T(8,128)}, u32[]{:S(2)}, u32[]{:S(2)}) async-start(f32[1,16,128,512]{3,1,0,2:T(8,128)} %copy.29), calls=%async_computation | async-start | bytes 8388608 | tf_op jit(solution)/shard_map/all_to_all | solution.py:64
  153.5 89.8 %all-to-all-done = f32[1,16,128,512]{3,1,0,2:T(8,128)} async-done(((f32[1,16,128,512]{3,1,0,2:T(8,128)}), f32[1,16,128,512]{3,1,0,2:T(8,128)}, u32[]{:S(2)}, u32[]{:S(2)}) %all-to-all-start) | async-done | bytes 4194336 | tf_op jit(solution)/shard_map/all_to_all | solution.py:64
  243.3 2.6 %multiply_reduce_fusion = f32[16,16,512]{2,0,1:T(8,128)S(1)} fusion(f32[8,16,16,512]{3,1,2,0:T(8,128)} %bitcast.5, f32[8,16,16]{1,2,0:T(8,128)S(1)} %get-tuple-element.144), kind=kLoop, calls=%fused_computation.22 | loop fusion | flops 1966080 | bytes 4726784 | tf_op jit(solution)/shard_map/reduce_sum | solution.py:70
  (63 shorter events, 13.0 us)
Async XLA Ops:
  7.4 10.9 %copy-start.1 = (s32[2]{0:T(128)S(1)}, s32[2]{0:T(128)}, u32[]{:S(2)}) copy-start(s32[2]{0:T(128)} %param.8) | copy-start | bytes 28
  7.4 10.8 %copy-start.2 = (s32[16]{0:T(128)S(1)}, s32[16]{0:T(128)}, u32[]{:S(2)}) copy-start(s32[16]{0:T(128)} %param.9) | copy-start | bytes 196
  7.4 68.8 %all-reduce.3.cloned.1.call-start = ((), (), s32[]{:S(2)}) async-start(), calls=%async_computation.4 | async-start | bytes 4718592 | tf_op jit(solution)/shard_map/psum | solution.py:16
  17.6 66.7 %all-gather.2.cloned.1.call-start = ((), (), s32[]{:S(2)}) async-start(), calls=%async_computation.3 | async-start | bytes 2654208 | tf_op jit(solution)/shard_map/all_gather | solution.py:38
  94.4 4.5 %copy-start = (bf16[2048,512]{1,0:T(8,128)(2,1)S(1)}, bf16[2048,512]{1,0:T(8,128)(2,1)}, u32[]{:S(2)}) copy-start(bf16[2048,512]{1,0:T(8,128)(2,1)} %get-tuple-element.243) | copy-start | bytes 6291460 | tf_op jit(solution)/shard_map/while
  101.3 4.5 %copy-start = (bf16[2048,512]{1,0:T(8,128)(2,1)S(1)}, bf16[2048,512]{1,0:T(8,128)(2,1)}, u32[]{:S(2)}) copy-start(bf16[2048,512]{1,0:T(8,128)(2,1)} %get-tuple-element.243) | copy-start | bytes 6291460 | tf_op jit(solution)/shard_map/while
  108.3 4.5 %copy-start = (bf16[2048,512]{1,0:T(8,128)(2,1)S(1)}, bf16[2048,512]{1,0:T(8,128)(2,1)}, u32[]{:S(2)}) copy-start(bf16[2048,512]{1,0:T(8,128)(2,1)} %get-tuple-element.243) | copy-start | bytes 6291460 | tf_op jit(solution)/shard_map/while
  115.3 4.5 %copy-start = (bf16[2048,512]{1,0:T(8,128)(2,1)S(1)}, bf16[2048,512]{1,0:T(8,128)(2,1)}, u32[]{:S(2)}) copy-start(bf16[2048,512]{1,0:T(8,128)(2,1)} %get-tuple-element.243) | copy-start | bytes 6291460 | tf_op jit(solution)/shard_map/while
  124.1 12.0 %all-to-all-start.1 = ((f32[8,1,256]{2,1,0:T(1,128)}), f32[8,1,256]{2,1,0:T(1,128)S(1)}, u32[]{:S(2)}, u32[]{:S(2)}) async-start(f32[8,1,256]{2,1,0:T(1,128)} %reshape.61), calls=%async_computation.1 | async-start | bytes 16384 | tf_op jit(solution)/shard_map/all_to_all | solution.py:65
  136.1 9.9 %all-to-all-start.2 = ((f32[8,1,256]{2,1,0:T(1,128)}), f32[8,1,256]{2,1,0:T(1,128)S(1)}, u32[]{:S(2)}, u32[]{:S(2)}) async-start(f32[8,1,256]{2,1,0:T(1,128)} %reshape.63), calls=%async_computation.2 | async-start | bytes 16384 | tf_op jit(solution)/shard_map/all_to_all | solution.py:66
  146.1 97.3 %all-to-all-start = ((f32[1,16,128,512]{3,1,0,2:T(8,128)}), f32[1,16,128,512]{3,1,0,2:T(8,128)}, u32[]{:S(2)}, u32[]{:S(2)}) async-start(f32[1,16,128,512]{3,1,0,2:T(8,128)} %copy.29), calls=%async_computation | async-start | bytes 8388608 | tf_op jit(solution)/shard_map/all_to_all | solution.py:64
Sparse Core Ops, SparseCore 0:
  17.7 58.3 all-reduce.2
Sparse Core Ops, SparseCore 1:
  20.3 54.4 all-gather.1
where the time goes:
time: 255 us; the launch traced here: 254 us
  waiting for transfers between devices  153 us (60%)
  local copies, waits for them, and re-layouts  29.3 us (11%)
  matrix products  22.7 us (9%)
  between operations  20 us (8%)
  starting transfers between devices  14.8 us (6%)
  other arithmetic  14 us (5%)
    all_to_all x1, waiting for transfers between devices, on_device(): lax.all_to_all(numerators[None], 'ctx', split_axis=2, concat_axis=0, tile...  89.8 us
    psum x1, waiting for transfers between devices, from_root(): return lax.psum(block, axis)  57.9 us
    dot_general x4, matrix products, partial_value(): jnp.einsum('qhw,kw->qhk', query_block, key_rows, preferred_element_type=j...  13.4 us
    unnamed x12, local copies, waits for them, and re-layouts  11.9 us
    dot_general x4, matrix products, partial_value(): jnp.einsum('qhk,kl->qhl', weights, value_rows, preferred_element_type=jnp...  9.3 us
    another operation x1, local copies, waits for them, and re-layouts, on_device(): numerators[None]  6.59 us
    all_to_all x1, starting transfers between devices, on_device(): lax.all_to_all(numerators[None], 'ctx', split_axis=2, concat_axis=0, tile...  5.93 us
    all_to_all x1, starting transfers between devices, on_device(): lax.all_to_all(peak_score[None], 'ctx', split_axis=2, concat_axis=0, tile...  5.51 us
  transfers between devices with their start and end apart: 5, of which 3 were waited for; matrix products, arithmetic and copies ran while one was open for 7% of the time, Pallas kernels for 0%

commit v1 on v0

--- a/solution.py
+++ b/solution.py
@@ -2,6 +2,7 @@
 import jax.numpy as jnp
 from jax import lax
 from jax.sharding import PartitionSpec as P
+from jax.lax import all_gather
 
 H = 128
 LAT = 512
@@ -13,7 +14,7 @@
 
 def from_root(block, axis, holder):
     block = jnp.where(lax.axis_index(axis) == holder, block, jnp.zeros_like(block))
-    return lax.psum(block, axis)
+    return all_gather(block, axis).sum(axis=0)
 
 
 def on_device(latents, queries, hot_ids, lengths):

time: 255 us -> 326 us (1.28)
  waiting for transfers between devices: 153 us -> 194 us
  other arithmetic: 14 us -> 33.9 us
  local copies, waits for them, and re-layouts: 29.3 us -> 40.9 us
    psum x1 -> x0, waiting for transfers between devices: 57.9 us -> none  [from_root(): return lax.psum(block, axis)]
    all_gather x0 -> x2, waiting for transfers between devices: none -> 51.9 us  [from_root(): return all_gather(block, axis).sum(axis=0)]
    all_gather x1, waiting for transfers between devices: 0.01 us -> 45.4 us  [on_device(): all_heads = lax.all_gather(queries, 'ctx', axis=1, tiled=True)]
    all_gather x0 -> x2, local copies, waits for them, and re-layouts: none -> 17.8 us  [from_root(): return all_gather(block, axis).sum(axis=0)]
    reduce_sum x0 -> x2, other arithmetic: none -> 17 us  [from_root(): return all_gather(block, axis).sum(axis=0)]
    unnamed x12 -> x15, local copies, waits for them, and re-layouts: 11.9 us -> 9.69 us
  transfers between devices with their start and end apart: 5 -> 6, of which waited for: 3 -> 5; matrix products, arithmetic and copies ran while one was open for 7% -> 12% of each run, Pallas kernels for 0% -> 0%
where the time goes in v1:
time: 326 us; the launch traced here: 325 us
  waiting for transfers between devices  194 us (60%)
  local copies, waits for them, and re-layouts  40.9 us (13%)
  other arithmetic  33.9 us (10%)
  matrix products  22.7 us (7%)
  between operations  18.7 us (6%)
  starting transfers between devices  14.9 us (5%)
    all_to_all x1, waiting for transfers between devices, on_device(): lax.all_to_all(numerators[None], 'ctx', split_axis=2, concat_axis=0, tile...  90.4 us
    all_gather x2, waiting for transfers between devices, from_root(): return all_gather(block, axis).sum(axis=0)  51.9 us
    all_gather x1, waiting for transfers between devices, on_device(): all_heads = lax.all_gather(queries, 'ctx', axis=1, tiled=True)  45.4 us
    all_gather x2, local copies, waits for them, and re-layouts, from_root(): return all_gather(block, axis).sum(axis=0)  17.8 us
    reduce_sum x2, other arithmetic, from_root(): return all_gather(block, axis).sum(axis=0)  17 us
    dot_general x4, matrix products, partial_value(): jnp.einsum('qhw,kw->qhk', query_block, key_rows, preferred_element_type=j...  13.4 us
    unnamed x15, local copies, waits for them, and re-layouts  9.69 us
    dot_general x4, matrix products, partial_value(): jnp.einsum('qhk,kl->qhl', weights, value_rows, preferred_element_type=jnp...  9.28 us
  transfers between devices with their start and end apart: 6, of which 5 were waited for; matrix products, arithmetic and copies ran while one was open for 12% of the time, Pallas kernels for 0%

profile of v1, /device:TPU:0, one launch (start us, length us, event | category | flops | bytes accessed | tf_op | source)
XLA Modules:
  0.0 325.3 jit_solution(10822426197529073168)
XLA Ops:
  14.1 3.7 %dynamic-slice_select_fusion.1 = (bf16[1024,576]{0,1:T(8,128)(2,1)}, bf16[1024,576]{0,1:T(8,128)(2,1)}) fusion(bf16[4096,576]{0,1:T(8,128)(2,1)} %param.6, s32[]{:T(128)S(6)} %select_n.48, pred[]{:T(512)S(6)} %eq.9, s32[]{:T(128)S(6)} %select_n.53, pred[]{:T(512)S(6)} %eq.10), kind=kLoop, calls=%fused_computation.28 | loop fusion | flops 1179648 | bytes 4718602 | tf_op jit(solution)/shard_map/jit(_where)/select_n | solution.py:16
  18.7 45.4 %all-gather.6.cloned.1.call-done = bf16[16,73728]{1,0:T(8,128)(2,1)} async-done(((bf16[16,9216]{1,0:T(8,128)(2,1)}), bf16[16,73728]{1,0:T(8,128)(2,1)}) %all-gather.6.cloned.1.call-update) | async-done | bytes 2359312 | tf_op jit(solution)/shard_map/all_gather | solution.py:39
  64.1 4.4 %reshape.58 = bf16[4,4,128,576]{3,2,1,0:T(8,128)(2,1)S(1)} reshape(bf16[16,73728]{1,0:T(8,128)(2,1)} %all-gather.6.cloned.1.call-done) | data formatting | bytes 4718592 | tf_op jit(solution)/shard_map/reshape | solution.py:41
  68.5 2.6 copy.24
  71.1 30.6 %all-gather.8.cloned.1.call-done = bf16[4096,576]{0,1:T(8,128)(2,1)} async-done(((bf16[1024,576]{0,1:T(8,128)(2,1)}), bf16[4096,576]{0,1:T(8,128)(2,1)}) %all-gather.8.cloned.1.call-update) | async-done | bytes 4718608 | tf_op jit(solution)/shard_map/all_gather | solution.py:17
  101.7 8.9 %reshape.59 = bf16[4,1024,576]{1,0,2:T(4,128)(2,1)} reshape(bf16[4096,576]{0,1:T(8,128)(2,1)} %all-gather.8.cloned.1.call-done) | data formatting | bytes 9437184 | tf_op jit(solution)/shard_map/all_gather | solution.py:17
  110.5 8.9 %reduce_sum.51 = bf16[1024,576]{0,1:T(8,128)(2,1)S(1)} reduce(bf16[4,1024,576]{1,0,2:T(4,128)(2,1)} %reshape.59, bf16[]{:T(256)} %constant.81.clone.1), dimensions={0}, to_apply=%region_0.1 | reduce | flops 1769472 | bytes 5898242 | tf_op jit(solution)/shard_map/reduce_sum | solution.py:17
  119.4 21.3 %all-gather.10.cloned.1.call-done = bf16[4096,576]{0,1:T(8,128)(2,1)} async-done(((bf16[1024,576]{0,1:T(8,128)(2,1)}), bf16[4096,576]{0,1:T(8,128)(2,1)}) %all-gather.10.cloned.1.call-update) | async-done | bytes 4718608 | tf_op jit(solution)/shard_map/all_gather | solution.py:17
  140.7 8.9 %reshape.60 = bf16[4,1024,576]{1,0,2:T(4,128)(2,1)} reshape(bf16[4096,576]{0,1:T(8,128)(2,1)} %all-gather.10.cloned.1.call-done) | data formatting | bytes 9437184 | tf_op jit(solution)/shard_map/all_gather | solution.py:17
  149.6 8.1 %reduce_sum.52 = bf16[1024,576]{0,1:T(8,128)(2,1)S(1)} reduce(bf16[4,1024,576]{1,0,2:T(4,128)(2,1)} %reshape.60, bf16[]{:T(256)} %constant.81.clone.1), dimensions={0}, to_apply=%region_1.2 | reduce | flops 1769472 | bytes 5898242 | tf_op jit(solution)/shard_map/reduce_sum | solution.py:17
  161.7 3.9 %copy.30 = bf16[2048,512]{1,0:T(8,128)(2,1)} copy(bf16[2048,512]{0,1:T(8,128)(2,1)} %fusion.18) | data formatting | bytes 4194304
  165.6 27.9 %while.15 = (s32[]{:T(128)}, f32[4,4,128,512]{3,2,1,0:T(8,128)}, f32[4,4,128]{2,1,0:T(4,128)S(1)}, f32[4,4,128]{2,1,0:T(4,128)S(1)}, s32[4,4]{1,0:T(4,128)S(1)},...) while((s32[]{:T(128)}, f32[4,4,128,512]{3,2,1,0:T(8,128)}, ...), condition=%wide.region_5.6_spmd.clone, body=%wide.region_2.5_spmd.clone.sunk | while | flops 2295342080 | bytes 27149504 | solution.py:60
  165.8 3.4 %select_reduce_fusion.2 = (f32[4,128]{1,0:T(4,128)S(1)}, f32[4,128,2048]{2,1,0:T(8,128)S(1)}) fusion(pred[4,2048]{1,0:T(4,128)(4,1)S(1)} %broadcast_compare_fusion.2, bf16[2048,576]{0,1:T(8,128)(2,1)S(1)} %get-tuple-element.240, bf16[4,4,128,576]{2,3,1,0:T(8,128)(2,1)} %get-tuple-element.239, s32[]{:T(128)} %get-tuple-element.224), kind=kOutput, calls=%fused_computation.3.clone.1 | convolution fusion | flops 1211104768 | bytes 7154176 | tf_op jit(solution)/shard_map/while/body/eval_jaxpr/qhw,kw->qhk/dot_general | solution.py:47
  172.7 3.4 %select_reduce_fusion.2 = (f32[4,128]{1,0:T(4,128)S(1)}, f32[4,128,2048]{2,1,0:T(8,128)S(1)}) fusion(pred[4,2048]{1,0:T(4,128)(4,1)S(1)} %broadcast_compare_fusion.2, bf16[2048,576]{0,1:T(8,128)(2,1)S(1)} %get-tuple-element.240, bf16[4,4,128,576]{2,3,1,0:T(8,128)(2,1)} %get-tuple-element.239, s32[]{:T(128)} %get-tuple-element.224), kind=kOutput, calls=%fused_computation.3.clone.1 | convolution fusion | flops 1211104768 | bytes 7154176 | tf_op jit(solution)/shard_map/while/body/eval_jaxpr/qhw,kw->qhk/dot_general | solution.py:47
  177.2 2.3 fusion.26
  179.7 3.4 %select_reduce_fusion.2 = (f32[4,128]{1,0:T(4,128)S(1)}, f32[4,128,2048]{2,1,0:T(8,128)S(1)}) fusion(pred[4,2048]{1,0:T(4,128)(4,1)S(1)} %broadcast_compare_fusion.2, bf16[2048,576]{0,1:T(8,128)(2,1)S(1)} %get-tuple-element.240, bf16[4,4,128,576]{2,3,1,0:T(8,128)(2,1)} %get-tuple-element.239, s32[]{:T(128)} %get-tuple-element.224), kind=kOutput, calls=%fused_computation.3.clone.1 | convolution fusion | flops 1211104768 | bytes 7154176 | tf_op jit(solution)/shard_map/while/body/eval_jaxpr/qhw,kw->qhk/dot_general | solution.py:47
  186.7 3.4 %select_reduce_fusion.2 = (f32[4,128]{1,0:T(4,128)S(1)}, f32[4,128,2048]{2,1,0:T(8,128)S(1)}) fusion(pred[4,2048]{1,0:T(4,128)(4,1)S(1)} %broadcast_compare_fusion.2, bf16[2048,576]{0,1:T(8,128)(2,1)S(1)} %get-tuple-element.240, bf16[4,4,128,576]{2,3,1,0:T(8,128)(2,1)} %get-tuple-element.239, s32[]{:T(128)} %get-tuple-element.224), kind=kOutput, calls=%fused_computation.3.clone.1 | convolution fusion | flops 1211104768 | bytes 7154176 | tf_op jit(solution)/shard_map/while/body/eval_jaxpr/qhw,kw->qhk/dot_general | solution.py:47
  195.5 5.5 %all-to-all-start.1 = ((f32[8,1,256]{2,1,0:T(1,128)}), f32[8,1,256]{2,1,0:T(1,128)S(1)}, u32[]{:S(2)}, u32[]{:S(2)}) async-start(f32[8,1,256]{2,1,0:T(1,128)} %reshape.63), calls=%async_computation.1 | async-start | bytes 16384 | tf_op jit(solution)/shard_map/all_to_all | solution.py:66
  202.5 5.0 %all-to-all-done.1 = f32[8,1,256]{2,1,0:T(1,128)S(1)} async-done(((f32[8,1,256]{2,1,0:T(1,128)}), f32[8,1,256]{2,1,0:T(1,128)S(1)}, u32[]{:S(2)}, u32[]{:S(2)}) %all-to-all-start.1) | async-done | bytes 8224 | tf_op jit(solution)/shard_map/all_to_all | solution.py:66
  207.5 3.6 %all-to-all-start.2 = ((f32[8,1,256]{2,1,0:T(1,128)}), f32[8,1,256]{2,1,0:T(1,128)S(1)}, u32[]{:S(2)}, u32[]{:S(2)}) async-start(f32[8,1,256]{2,1,0:T(1,128)} %reshape.65), calls=%async_computation.2 | async-start | bytes 16384 | tf_op jit(solution)/shard_map/all_to_all | solution.py:67
  211.1 6.5 %copy.29 = f32[1,16,128,512]{3,1,0,2:T(8,128)} copy(f32[1,16,128,512]{3,2,1,0:T(8,128)} %bitcast.2) | data formatting | bytes 8388608 | tf_op jit(solution)/shard_map/broadcast_in_dim;reshape | solution.py:65
  217.6 5.7 %all-to-all-start = ((f32[1,16,128,512]{3,1,0,2:T(8,128)}), f32[1,16,128,512]{3,1,0,2:T(8,128)}, u32[]{:S(2)}, u32[]{:S(2)}) async-start(f32[1,16,128,512]{3,1,0,2:T(8,128)} %copy.29), calls=%async_computation | async-start | bytes 8388608 | tf_op jit(solution)/shard_map/all_to_all | solution.py:65
  224.9 90.4 %all-to-all-done = f32[1,16,128,512]{3,1,0,2:T(8,128)} async-done(((f32[1,16,128,512]{3,1,0,2:T(8,128)}), f32[1,16,128,512]{3,1,0,2:T(8,128)}, u32[]{:S(2)}, u32[]{:S(2)}) %all-to-all-start) | async-done | bytes 4194336 | tf_op jit(solution)/shard_map/all_to_all | solution.py:65
  315.3 2.6 multiply_reduce_fusion
  (73 shorter events, 24.8 us)
Async XLA Ops:
  6.5 12.2 %copy-start.3 = (s32[2]{0:T(128)S(1)}, s32[2]{0:T(128)}, u32[]{:S(2)}) copy-start(s32[2]{0:T(128)} %param.8) | copy-start | bytes 28
  6.5 12.1 %copy-start.4 = (s32[16]{0:T(128)S(1)}, s32[16]{0:T(128)}, u32[]{:S(2)}) copy-start(s32[16]{0:T(128)} %param.9) | copy-start | bytes 196
  6.5 57.6 %all-gather.6.cloned.1.call-start = ((), (), s32[]{:S(2)}) async-start(), calls=%async_computation.3 | async-start | bytes 2654208 | tf_op jit(solution)/shard_map/all_gather | solution.py:39
  7.3 94.4 %all-gather.8.cloned.1.call-start = ((), (), s32[]{:S(2)}) async-start(), calls=%async_computation.4 | async-start | bytes 5898240 | tf_op jit(solution)/shard_map/all_gather | solution.py:17
  17.8 122.9 %all-gather.10.cloned.1.call-start = ((), (), s32[]{:S(2)}) async-start(), calls=%async_computation.5 | async-start | bytes 5898240 | tf_op jit(solution)/shard_map/all_gather | solution.py:17
  157.7 1.0 copy-start
  161.6 4.0 %copy-start.2 = (f32[4,4,128]{2,1,0:T(4,128)S(1)}, f32[4,4,128]{2,1,0:T(4,128)}, u32[]{:S(2)}) copy-start(f32[4,4,128]{2,1,0:T(4,128)} %custom-call.2) | copy-start | bytes 24580
  165.8 4.5 %copy-start.1 = (bf16[2048,512]{1,0:T(8,128)(2,1)S(1)}, bf16[2048,512]{1,0:T(8,128)(2,1)}, u32[]{:S(2)}) copy-start(bf16[2048,512]{1,0:T(8,128)(2,1)} %get-tuple-element.241) | copy-start | bytes 6291460 | tf_op jit(solution)/shard_map/while
  172.7 4.5 %copy-start.1 = (bf16[2048,512]{1,0:T(8,128)(2,1)S(1)}, bf16[2048,512]{1,0:T(8,128)(2,1)}, u32[]{:S(2)}) copy-start(bf16[2048,512]{1,0:T(8,128)(2,1)} %get-tuple-element.241) | copy-start | bytes 6291460 | tf_op jit(solution)/shard_map/while
  179.7 4.5 %copy-start.1 = (bf16[2048,512]{1,0:T(8,128)(2,1)S(1)}, bf16[2048,512]{1,0:T(8,128)(2,1)}, u32[]{:S(2)}) copy-start(bf16[2048,512]{1,0:T(8,128)(2,1)} %get-tuple-element.241) | copy-start | bytes 6291460 | tf_op jit(solution)/shard_map/while
  186.7 4.5 %copy-start.1 = (bf16[2048,512]{1,0:T(8,128)(2,1)S(1)}, bf16[2048,512]{1,0:T(8,128)(2,1)}, u32[]{:S(2)}) copy-start(bf16[2048,512]{1,0:T(8,128)(2,1)} %get-tuple-element.241) | copy-start | bytes 6291460 | tf_op jit(solution)/shard_map/while
  195.5 12.0 %all-to-all-start.1 = ((f32[8,1,256]{2,1,0:T(1,128)}), f32[8,1,256]{2,1,0:T(1,128)S(1)}, u32[]{:S(2)}, u32[]{:S(2)}) async-start(f32[8,1,256]{2,1,0:T(1,128)} %reshape.63), calls=%async_computation.1 | async-start | bytes 16384 | tf_op jit(solution)/shard_map/all_to_all | solution.py:66
  207.5 10.1 %all-to-all-start.2 = ((f32[8,1,256]{2,1,0:T(1,128)}), f32[8,1,256]{2,1,0:T(1,128)S(1)}, u32[]{:S(2)}, u32[]{:S(2)}) async-start(f32[8,1,256]{2,1,0:T(1,128)} %reshape.65), calls=%async_computation.2 | async-start | bytes 16384 | tf_op jit(solution)/shard_map/all_to_all | solution.py:67
  217.6 97.7 %all-to-all-start = ((f32[1,16,128,512]{3,1,0,2:T(8,128)}), f32[1,16,128,512]{3,1,0,2:T(8,128)}, u32[]{:S(2)}, u32[]{:S(2)}) async-start(f32[1,16,128,512]{3,1,0,2:T(8,128)} %copy.29), calls=%async_computation | async-start | bytes 8388608 | tf_op jit(solution)/shard_map/all_to_all | solution.py:65
Sparse Core Ops, SparseCore 0:
  9.5 54.5 all-gather.5
  65.7 35.9 all-gather.7
  103.2 37.4 all-gather.9
